TPU v7x, 32 devices: a whole 2x2x4 slice. The times are simulated.
32 devices in a mesh: space: 16 (over z, y, core), tensor: 2 (over x).
Axes of the slice: x: 2, y: 2, z: 4, core: 2. Of those that a mesh axis runs over, the one named last changes fastest.
Arguments:
- tokens: bfloat16 [14336, 1024], P('space', 'tensor'), may hold values from -6 to 6
- first_weight: bfloat16 [1024, 1024], P(None, 'tensor'), may hold values from -0.1875 to 0.1875
- second_weight: bfloat16 [1024, 1024], P(None, 'tensor'), may hold values from -0.1875 to 0.1875
- head_weight: bfloat16 [352, 1024], P('tensor'), may hold values from -0.1875 to 0.1875
- targets: float32 [352, 14336], P('tensor', 'space'), may hold values from -6 to 6
- land_mask: int32 [4, 14336], P(None, 'space'), may hold values from 0 to 1, as said below
- variable_kind: int32 [88], P('tensor'), may hold values from 0 to 2
- loss_scale: float32 [], replicated, may hold values from 630784 to 5046272
Outputs:
- loss: float32 [], replicated
- token_grad: float32 [14336, 1024], P('space', 'tensor')
- first_grad: float32 [1024, 1024], P('space', 'tensor')
- second_grad: float32 [1024, 1024], P('space', 'tensor')
- head_grad: float32 [352, 1024], P('tensor', 'space')
Inputs may be any that keep to these rules, and one draw needn't show every extreme that they name: `land_mask`: every aligned group of 8 entries along the last dimension holds at least one 1 and one 0. `variable_kind`: 0 scores a variable on all cells, 1 on land cells, 2 on ocean cells.
All inputs are finite; a program needn't handle non-finite values.
Results may differ from a plain program's by a relative error of at most 0.0056.
Values may be sent and summed in bfloat16 or wider, within the bound.
A program may use at most 64 MiB of HBM per device.

v0:
```python
import math
import jax
import jax.numpy as jnp
from jax import lax
from jax.sharding import PartitionSpec as P

V = 88
PP = 4
PROW_DEV = 4
LONP = 224


def slope(z):
    cdf = 0.5 * (1.0 + lax.erf(z / math.sqrt(2.0)))
    return cdf + z * jnp.exp(-0.5 * z * z) / math.sqrt(2.0 * math.pi)


def column_folder(weights, piece):
    return lax.dot_general(
        piece, weights, (((1,), (1,)), ((), ())), preferred_element_type=jnp.float32
    )


def row_folder(weights, piece):
    return lax.dot_general(
        piece, weights, (((0,), (0,)), ((), ())), preferred_element_type=jnp.float32
    )


def per_device(
    tokens, first_weight, second_weight, head_weight, targets, land_mask, variable_kind, loss_scale
):
    count = tokens.shape[0]
    width = first_weight.shape[1]
    kinds = head_weight.shape[0] // PP
    rows_first, rows_second = (
        lax.all_to_all(first_weight, "tensor", split_axis=0, concat_axis=1, tiled=True),
        lax.all_to_all(second_weight, "tensor", split_axis=0, concat_axis=1, tiled=True),
    )
    head_cols = lax.all_to_all(head_weight, "tensor", split_axis=1, concat_axis=0, tiled=True)
    position = lax.axis_index("space") * count + jnp.arange(count, dtype=jnp.int32)
    cell = jnp.arange(PP, dtype=jnp.int32)
    lat_row = 2 * (position // LONP)[None, :] + (cell // 2)[:, None]
    nlat = 2 * PROW_DEV * lax.axis_size("space")
    cell_weight = jnp.cos(math.pi / 2.0 * (lat_row.astype(jnp.float32) + 0.5) / nlat)
    land = land_mask.astype(jnp.float32)
    kind = variable_kind[:, None, None]
    valid = jnp.where(kind == 0, 1.0, jnp.where(kind == 1, land[None], 1.0 - land[None]))
    masked = cell_weight[None] * valid
    local_weight = jnp.sum(masked, axis=(1, 2))
    weight_sum = lax.psum(local_weight, "space")
    full_in = lax.all_gather(tokens, "tensor", axis=1, tiled=True)
    pre_one = jnp.dot(full_in, first_weight, preferred_element_type=jnp.float32)
    hidden_one = jax.nn.gelu(pre_one, approximate=False).astype(jnp.bfloat16)
    full_one = lax.all_gather(hidden_one, "tensor", axis=1, tiled=True)
    pre_two = jnp.dot(full_one, second_weight, preferred_element_type=jnp.float32)
    hidden_two = jax.nn.gelu(pre_two, approximate=False).astype(jnp.bfloat16)
    full_two = lax.all_gather(hidden_two, "tensor", axis=1, tiled=True)
    predicted = lax.dot_general(
        head_weight, full_two, (((1,), (1,)), ((), ())), preferred_element_type=jnp.float32
    )
    error = predicted.reshape(kinds, PP, count) - targets.reshape(kinds, PP, count)
    local_error = jnp.sum(masked * error * error, axis=(1, 2))
    error_sum = lax.psum(local_error, "space")
    root = jnp.sqrt(error_sum / weight_sum + 1e-06)
    loss = lax.psum(jnp.sum(root), "tensor") / V
    coef = loss_scale / (V * root * weight_sum)
    grad_pred = (
        (coef[:, None, None] * masked * error).reshape(kinds * PP, count).astype(jnp.bfloat16)
    )
    back_two = row_folder(head_cols, lax.all_gather(grad_pred, "tensor", axis=0, tiled=True))
    head_term = jnp.dot(grad_pred, full_two, preferred_element_type=jnp.float32)
    head_grad = lax.psum_scatter(head_term, "space", scatter_dimension=1, tiled=True)
    grad_two = (back_two * slope(pre_two)).astype(jnp.bfloat16)
    back_one = column_folder(rows_second, lax.all_gather(grad_two, "tensor", axis=1, tiled=True))
    grad_one = (back_one * slope(pre_one)).astype(jnp.bfloat16)
    joined = lax.psum_scatter(
        jnp.concatenate(
            [
                lax.dot_general(
                    full_one, grad_two, (((0,), (0,)), ((), ())), preferred_element_type=jnp.float32
                ),
                lax.dot_general(
                    full_in, grad_one, (((0,), (0,)), ((), ())), preferred_element_type=jnp.float32
                ),
            ],
            axis=1,
        ),
        "space",
        scatter_dimension=0,
        tiled=True,
    )
    second_grad = joined[:, :width]
    first_grad = joined[:, width:]
    token_grad = column_folder(rows_first, lax.all_gather(grad_one, "tensor", axis=1, tiled=True))
    return (loss, token_grad, first_grad, second_grad, head_grad)


def solution(mesh):
    return jax.shard_map(
        per_device,
        mesh=mesh,
        in_specs=(
            P("space", "tensor"),
            P(None, "tensor"),
            P(None, "tensor"),
            P("tensor", None),
            P("tensor", "space"),
            P(None, "space"),
            P("tensor"),
            P(),
        ),
        out_specs=(
            P(),
            P("space", "tensor"),
            P("space", "tensor"),
            P("space", "tensor"),
            P("tensor", "space"),
        ),
        check_vma=False,
    )
```

profile of v0, /device:TPU:0, one launch (start us, length us, event | category | flops | bytes accessed | tf_op | source)
XLA Modules:
  0.0 390.4 jit_solution(11387166332372937541)
XLA Ops:
  8.0 34.5 %all-gather.6.cloned.1.call-done = bf16[896,1024]{1,0:T(8,128)(2,1)} async-done(((bf16[896,512]{1,0:T(8,128)(2,1)}), bf16[896,1024]{1,0:T(8,128)(2,1)}) %all-gather.6.cloned.1.call-update) | async-done | bytes 1835024 | tf_op jit(solution)/shard_map/all_gather | solution.py:52
  42.4 8.0 %fusion.2 = (bf16[896,512]{1,0:T(8,128)(2,1)}, f32[896,512]{1,0:T(8,128)}) fusion(bf16[896,1024]{1,0:T(8,128)(2,1)} %all-gather.6.cloned.1.call-done, bf16[1024,512]{1,0:T(8,128)(2,1)} %param.9), kind=kOutput, calls=%fused_computation.7 | convolution fusion | flops 969342976 | bytes 5636096 | tf_op jit(solution)/shard_map/dot_general | solution.py:53
  50.5 30.2 %all-gather.8.cloned.1.call-done = bf16[896,1024]{1,0:T(8,128)(2,1)} async-done(((bf16[896,512]{1,0:T(8,128)(2,1)}), bf16[896,1024]{1,0:T(8,128)(2,1)}) %all-gather.8.cloned.1.call-update) | async-done | bytes 1835024 | tf_op jit(solution)/shard_map/all_gather | solution.py:55
  80.7 7.5 %fusion.5 = (bf16[896,512]{1,0:T(8,128)(2,1)}, f32[896,512]{1,0:T(8,128)}) fusion(bf16[896,1024]{1,0:T(8,128)(2,1)} %all-gather.8.cloned.1.call-done, bf16[1024,512]{1,0:T(8,128)(2,1)S(1)} %copy-done.4), kind=kOutput, calls=%fused_computation.10 | convolution fusion | flops 969342976 | bytes 5636096 | tf_op jit(solution)/shard_map/dot_general | solution.py:56
  89.0 4.2 %all-to-all-start = ((bf16[176,2,512]{2,0,1:T(8,128)(2,1)}), bf16[176,2,512]{2,0,1:T(8,128)(2,1)}, u32[]{:S(2)}, u32[]{:S(2)}) async-start(bf16[176,2,512]{2,0,1:T(8,128)(2,1)} %bitcast.37), calls=%async_computation | async-start | bytes 720896 | tf_op jit(solution)/shard_map/all_to_all | solution.py:40
  96.3 23.1 %all-gather.10.cloned.1.call-done = bf16[896,1024]{1,0:T(8,128)(2,1)} async-done(((bf16[896,512]{1,0:T(8,128)(2,1)}), bf16[896,1024]{1,0:T(8,128)(2,1)}) %all-gather.10.cloned.1.call-update) | async-done | bytes 1835024 | tf_op jit(solution)/shard_map/all_gather | solution.py:58
  119.4 2.6 fusion.33
  122.2 33.2 %all-reduce = (f32[44]{0:T(128)S(1)}, f32[44]{0:T(128)S(1)}) all-reduce(f32[44]{0:T(128)S(1)} %reduce_sum.36, f32[44]{0:T(128)S(1)} %multiply_reduce_fusion), channel_id=1, replica_groups=mesh['space'=16,'tensor'=2] {'space'}, use_global_device_ids=true, to_apply=%region_2.3 | all-reduce | flops 88 | bytes 704 | tf_op jit(solution)/shard_map/psum | solution.py:64
  155.8 7.6 %all_gather.21 = bf16[352,896]{1,0:T(8,128)(2,1)S(1)} all-gather(bf16[176,896]{1,0:T(8,128)(2,1)S(1)} %multiply_convert_fusion), channel_id=1, replica_groups=mesh['space'=16,'tensor'=2] {'tensor'}, dimensions={0}, use_global_device_ids=true | all-gather | bytes 946176 | tf_op jit(solution)/shard_map/all_gather | solution.py:71
  163.4 3.7 fusion.11
  167.2 22.7 %all_to_all.57 = bf16[2,512,512]{2,1,0:T(8,128)(2,1)S(1)} all-to-all(bf16[2,512,512]{2,1,0:T(8,128)(2,1)S(1)} %bitcast.41), channel_id=1, replica_groups=mesh['space'=16,'tensor'=2] {'tensor'}, dimensions={0} | all-to-all | bytes 2097152 | tf_op jit(solution)/shard_map/all_to_all | solution.py:38
  190.4 8.6 %all-gather.12.cloned.1.call-done = bf16[896,1024]{1,0:T(8,128)(2,1)} async-done(((bf16[896,512]{1,0:T(8,128)(2,1)}), bf16[896,1024]{1,0:T(8,128)(2,1)}) %all-gather.12.cloned.1.call-update) | async-done | bytes 1835024 | tf_op jit(solution)/shard_map/all_gather | solution.py:75
  199.0 4.6 %fusion.17 = bf16[896,512]{1,0:T(8,128)(2,1)} fusion(f32[896,512]{1,0:T(8,128)} %get-tuple-element.36, bf16[896,1024]{1,0:T(8,128)(2,1)} %all-gather.12.cloned.1.call-done, bf16[512,1024]{0,1:T(8,128)(2,1)S(1)} %bitcast.44), kind=kOutput, calls=%fused_computation.22 | convolution fusion | flops 944111616 | bytes 5636096 | tf_op jit(solution)/shard_map/dot_general | solution.py:19
  203.7 3.2 fusion.38
  208.1 2.5 pad_maximum_fusion
  210.6 5.5 %copy.27 = f32[1024,1024]{1,0:T(8,128)} copy(f32[1024,1024]{0,1:T(8,128)} %pad_maximum_fusion) | data formatting | bytes 8388608
  216.2 3.7 all-to-all-start.2
  220.0 1.9 fusion.39
  222.5 22.4 %all-to-all-done.2 = bf16[2,512,512]{2,1,0:T(8,128)(2,1)S(1)} async-done(((bf16[2,512,512]{2,1,0:T(8,128)(2,1)}), bf16[2,512,512]{2,1,0:T(8,128)(2,1)S(1)}, u32[]{:S(2)}, u32[]{:S(2)}) %all-to-all-start.2) | async-done | bytes 1048608 | tf_op jit(solution)/shard_map/all_to_all | solution.py:37
  245.4 5.6 %psum.23 = f32[]{:T(128)} all-reduce(f32[]{:T(128)} %reduce_sum.38), channel_id=1, replica_groups=mesh['space'=16,'tensor'=2] {'tensor'}, use_global_device_ids=true, to_apply=%region_6.7 | all-reduce | flops 1 | bytes 8 | tf_op jit(solution)/shard_map/psum | solution.py:66
  251.7 3.9 fusion.37
  255.5 66.0 %reduce-scatter.7.cloned.1.call-done = f32[64,1024]{1,0:T(8,128)} async-done(((f32[1024,1024]{1,0:T(8,128)}), f32[64,1024]{1,0:T(8,128)}) %reduce-scatter.7.cloned.1.call-update) | async-done | bytes 262160
  321.5 1.7 fusion.36
  323.2 59.2 %reduce-scatter.5.cloned.1.call-done = f32[176,64]{0,1:T(8,128)} async-done(((f32[176,1024]{0,1:T(8,128)}), f32[176,64]{0,1:T(8,128)}) %reduce-scatter.5.cloned.1.call-update) | async-done | bytes 45072 | tf_op jit(solution)/shard_map/reduce_scatter | solution.py:73
  (59 shorter events, 7.7 us)
Async XLA Ops:
  7.2 35.2 %all-gather.6.cloned.1.call-start = ((), (), s32[]{:S(2)}) async-start(), calls=%async_computation.5 | async-start | bytes 2752512 | tf_op jit(solution)/shard_map/all_gather | solution.py:52
  7.9 72.8 %copy-start.4 = (bf16[1024,512]{1,0:T(8,128)(2,1)S(1)}, bf16[1024,512]{1,0:T(8,128)(2,1)}, u32[]{:S(2)}) copy-start(bf16[1024,512]{1,0:T(8,128)(2,1)} %param.10) | copy-start | bytes 3145732
  7.9 72.8 %all-gather.8.cloned.1.call-start = ((), (), s32[]{:S(2)}) async-start(), calls=%async_computation.6 | async-start | bytes 2752512 | tf_op jit(solution)/shard_map/all_gather | solution.py:55
  50.4 37.8 %copy-start.3 = (bf16[176,1024]{1,0:T(8,128)(2,1)S(1)}, bf16[176,1024]{1,0:T(8,128)(2,1)}, u32[]{:S(2)}) copy-start(bf16[176,1024]{1,0:T(8,128)(2,1)} %param.11) | copy-start | bytes 1081348
  50.4 69.0 %all-gather.10.cloned.1.call-start = ((), (), s32[]{:S(2)}) async-start(), calls=%async_computation.7 | async-start | bytes 2752512 | tf_op jit(solution)/shard_map/all_gather | solution.py:58
  88.2 5.0 %copy-start.6 = (s32[4,896]{1,0:T(4,128)S(1)}, s32[4,896]{1,0:T(4,128)}, u32[]{:S(2)}) copy-start(s32[4,896]{1,0:T(4,128)} %param.13) | copy-start | bytes 43012
  89.0 74.4 %all-to-all-start = ((bf16[176,2,512]{2,0,1:T(8,128)(2,1)}), bf16[176,2,512]{2,0,1:T(8,128)(2,1)}, u32[]{:S(2)}, u32[]{:S(2)}) async-start(bf16[176,2,512]{2,0,1:T(8,128)(2,1)} %bitcast.37), calls=%async_computation | async-start | bytes 720896 | tf_op jit(solution)/shard_map/all_to_all | solution.py:40
  93.2 105.8 %all-gather.12.cloned.1.call-start = ((), (), s32[]{:S(2)}) async-start(), calls=%async_computation.8 | async-start | bytes 2752512 | tf_op jit(solution)/shard_map/all_gather | solution.py:75
  93.8 0.7 copy-start.7
  163.4 3.8 copy-start.5
  167.2 84.5 %all-gather.14.cloned.1.call-start = ((), (), s32[]{:S(2)}) async-start(), calls=%async_computation.9 | async-start | bytes 2752512 | tf_op jit(solution)/shard_map/all_gather | solution.py:95
  203.6 3.2 copy-start.1
  203.6 3.2 copy-start.2
  203.6 117.9 %reduce-scatter.7.cloned.1.call-start = ((), (), s32[]{:S(2)}) async-start(), calls=%async_computation.11 | async-start | bytes 4456448
  216.2 3.8 copy-start
  216.2 28.7 %all-to-all-start.2 = ((bf16[2,512,512]{2,1,0:T(8,128)(2,1)}), bf16[2,512,512]{2,1,0:T(8,128)(2,1)S(1)}, u32[]{:S(2)}, u32[]{:S(2)}) async-start(bf16[2,512,512]{2,1,0:T(8,128)(2,1)} %bitcast.42), calls=%async_computation.2 | async-start | bytes 2097152 | tf_op jit(solution)/shard_map/all_to_all | solution.py:37
  219.9 162.5 %reduce-scatter.5.cloned.1.call-start = ((), (), s32[]{:S(2)}) async-start(), calls=%async_computation.10 | async-start | bytes 1114112 | tf_op jit(solution)/shard_map/reduce_scatter | solution.py:73
Sparse Core Ops, SparseCore 0:
  9.5 32.8 all-gather.5
  50.5 30.1 all-gather.7
  88.3 31.0 all-gather.9
  167.3 31.6 all-gather.11
  203.7 40.9 all-gather.13
  248.5 72.9 reduce-scatter.6
  325.7 56.6 reduce-scatter.4
where the time goes:
time: 391 us; the launch traced here: 390 us
  waiting for transfers between devices  245 us (63%)
  blocking collectives  69.1 us (18%)
  matrix products  36.5 us (9%)
  between operations  16.8 us (4%)
  local copies, waits for them, and re-layouts  10.7 us (3%)
  starting transfers between devices  8.16 us (2%)
  other arithmetic  4.37 us (1%)
    unnamed x8, waiting for transfers between devices  66.7 us
    reduce_scatter x1, waiting for transfers between devices, per_device(): lax.psum_scatter(head_term, 'space', scatter_dimension=1, tiled=True)  59.2 us
    all_gather x1, waiting for transfers between devices, per_device(): full_in = lax.all_gather(tokens, 'tensor', axis=1, tiled=True)  34.5 us
    psum x1, blocking collectives, per_device(): error_sum = lax.psum(local_error, 'space')  33.2 us
    all_gather x1, waiting for transfers between devices, per_device(): full_one = lax.all_gather(hidden_one, 'tensor', axis=1, tiled=True)  30.2 us
    all_gather x1, waiting for transfers between devices, per_device(): full_two = lax.all_gather(hidden_two, 'tensor', axis=1, tiled=True)  23.1 us
    all_to_all x1, blocking collectives, per_device(): lax.all_to_all(second_weight, 'tensor', split_axis=0, concat_axis=1, tile...  22.7 us
    all_to_all x1, waiting for transfers between devices, per_device(): lax.all_to_all(first_weight, 'tensor', split_axis=0, concat_axis=1, tiled...  22.4 us
  transfers between devices with their start and end apart: 9, of which 7 were waited for; matrix products, arithmetic and copies ran while one was open for 7% of the time, Pallas kernels for 0%

commit v1 on v0

--- a/solution.py
+++ b/solution.py
@@ -49,7 +49,7 @@
     masked = cell_weight[None] * valid
     local_weight = jnp.sum(masked, axis=(1, 2))
     weight_sum = lax.psum(local_weight, "space")
-    full_in = lax.all_gather(tokens, "tensor", axis=1, tiled=True)
+    full_in = jnp.concatenate(lax.all_gather(tokens, "tensor"), axis=1)
     pre_one = jnp.dot(full_in, first_weight, preferred_element_type=jnp.float32)
     hidden_one = jax.nn.gelu(pre_one, approximate=False).astype(jnp.bfloat16)
     full_one = lax.all_gather(hidden_one, "tensor", axis=1, tiled=True)

time: 391 us -> 394 us (level)
  no operation moved by 1% of the time
where the time goes in v1:
time: 394 us
  waiting for transfers between devices  245 us (62%)
  blocking collectives  69.3 us (18%)
  matrix products  36.7 us (9%)
  between operations  16.8 us (4%)
  local copies, waits for them, and re-layouts  13.6 us (3%)
  starting transfers between devices  8.16 us (2%)
  other arithmetic  4.38 us (1%)
    unnamed x8, waiting for transfers between devices  66.7 us
    reduce_scatter x1, waiting for transfers between devices, per_device(): lax.psum_scatter(head_term, 'space', scatter_dimension=1, tiled=True)  59.2 us
    all_gather x1, waiting for transfers between devices, per_device(): full_in = jnp.concatenate(lax.all_gather(tokens, 'tensor'), axis=1)  34.5 us
    psum x1, blocking collectives, per_device(): error_sum = lax.psum(local_error, 'space')  33.2 us
    all_gather x1, waiting for transfers between devices, per_device(): full_one = lax.all_gather(hidden_one, 'tensor', axis=1, tiled=True)  30.2 us
    all_gather x1, waiting for transfers between devices, per_device(): full_two = lax.all_gather(hidden_two, 'tensor', axis=1, tiled=True)  23.1 us
    all_to_all x1, blocking collectives, per_device(): lax.all_to_all(second_weight, 'tensor', split_axis=0, concat_axis=1, tile...  22.7 us
    all_to_all x1, waiting for transfers between devices, per_device(): lax.all_to_all(first_weight, 'tensor', split_axis=0, concat_axis=1, tiled...  22.4 us
  transfers between devices with their start and end apart: 9, of which 7 were waited for; matrix products, arithmetic and copies ran while one was open for 7% of the time, Pallas kernels for 0%

profile of v1, /device:TPU:0, one launch (start us, length us, event | category | flops | bytes accessed | tf_op | source)
XLA Modules:
  0.0 393.6 jit_solution(17771153555626869735)
XLA Ops:
  7.9 34.5 %all-gather.15.cloned.1.call-done = bf16[1792,512]{1,0:T(8,128)(2,1)} async-done(((bf16[896,512]{1,0:T(8,128)(2,1)}), bf16[1792,512]{1,0:T(8,128)(2,1)}) %all-gather.15.cloned.1.call-update) | async-done | bytes 1835024 | tf_op jit(solution)/shard_map/all_gather | solution.py:52
  42.4 2.9 copy.23
  45.3 8.1 %fusion.2 = (bf16[896,512]{1,0:T(8,128)(2,1)}, f32[896,512]{1,0:T(8,128)}) fusion(bf16[896,1024]{0,1:T(8,128)(2,1)S(1)} %bitcast.44, bf16[1024,512]{1,0:T(8,128)(2,1)} %param.9), kind=kOutput, calls=%fused_computation.7 | convolution fusion | flops 969342976 | bytes 5636096 | tf_op jit(solution)/shard_map/dot_general | solution.py:53
  53.5 30.2 %all-gather.7.cloned.1.call-done = bf16[896,1024]{1,0:T(8,128)(2,1)} async-done(((bf16[896,512]{1,0:T(8,128)(2,1)}), bf16[896,1024]{1,0:T(8,128)(2,1)}) %all-gather.7.cloned.1.call-update) | async-done | bytes 1835024 | tf_op jit(solution)/shard_map/all_gather | solution.py:55
  83.7 7.5 %fusion.5 = (bf16[896,512]{1,0:T(8,128)(2,1)}, f32[896,512]{1,0:T(8,128)}) fusion(bf16[896,1024]{1,0:T(8,128)(2,1)} %all-gather.7.cloned.1.call-done, bf16[1024,512]{1,0:T(8,128)(2,1)S(1)} %copy-done.4), kind=kOutput, calls=%fused_computation.10 | convolution fusion | flops 969342976 | bytes 5636096 | tf_op jit(solution)/shard_map/dot_general | solution.py:56
  92.0 4.1 %all-to-all-start = ((bf16[176,2,512]{2,0,1:T(8,128)(2,1)}), bf16[176,2,512]{2,0,1:T(8,128)(2,1)}, u32[]{:S(2)}, u32[]{:S(2)}) async-start(bf16[176,2,512]{2,0,1:T(8,128)(2,1)} %bitcast.41), calls=%async_computation | async-start | bytes 720896 | tf_op jit(solution)/shard_map/all_to_all | solution.py:40
  99.3 23.1 %all-gather.9.cloned.1.call-done = bf16[896,1024]{1,0:T(8,128)(2,1)} async-done(((bf16[896,512]{1,0:T(8,128)(2,1)}), bf16[896,1024]{1,0:T(8,128)(2,1)}) %all-gather.9.cloned.1.call-update) | async-done | bytes 1835024 | tf_op jit(solution)/shard_map/all_gather | solution.py:58
  122.4 2.6 fusion.33
  125.2 33.2 %all-reduce = (f32[44]{0:T(128)S(1)}, f32[44]{0:T(128)S(1)}) all-reduce(f32[44]{0:T(128)S(1)} %reduce_sum.36, f32[44]{0:T(128)S(1)} %multiply_reduce_fusion), channel_id=1, replica_groups=mesh['space'=16,'tensor'=2] {'space'}, use_global_device_ids=true, to_apply=%region_2.3 | all-reduce | flops 88 | bytes 704 | tf_op jit(solution)/shard_map/psum | solution.py:64
  158.8 7.8 %all_gather.25 = bf16[352,896]{1,0:T(8,128)(2,1)S(1)} all-gather(bf16[176,896]{1,0:T(8,128)(2,1)S(1)} %multiply_convert_fusion), channel_id=1, replica_groups=mesh['space'=16,'tensor'=2] {'tensor'}, dimensions={0}, use_global_device_ids=true | all-gather | bytes 946176 | tf_op jit(solution)/shard_map/all_gather | solution.py:71
  166.6 3.7 fusion.11
  170.4 22.7 %all_to_all.57 = bf16[2,512,512]{2,1,0:T(8,128)(2,1)S(1)} all-to-all(bf16[2,512,512]{2,1,0:T(8,128)(2,1)S(1)} %bitcast.48), channel_id=1, replica_groups=mesh['space'=16,'tensor'=2] {'tensor'}, dimensions={0} | all-to-all | bytes 2097152 | tf_op jit(solution)/shard_map/all_to_all | solution.py:38
  193.7 8.5 %all-gather.11.cloned.1.call-done = bf16[896,1024]{1,0:T(8,128)(2,1)} async-done(((bf16[896,512]{1,0:T(8,128)(2,1)}), bf16[896,1024]{1,0:T(8,128)(2,1)}) %all-gather.11.cloned.1.call-update) | async-done | bytes 1835024 | tf_op jit(solution)/shard_map/all_gather | solution.py:75
  202.2 4.6 %fusion.17 = bf16[896,512]{1,0:T(8,128)(2,1)} fusion(f32[896,512]{1,0:T(8,128)} %get-tuple-element.36, bf16[896,1024]{1,0:T(8,128)(2,1)} %all-gather.11.cloned.1.call-done, bf16[512,1024]{0,1:T(8,128)(2,1)S(1)} %bitcast.51), kind=kOutput, calls=%fused_computation.22 | convolution fusion | flops 944111616 | bytes 5636096 | tf_op jit(solution)/shard_map/dot_general | solution.py:19
  206.9 3.2 fusion.38
  211.4 2.5 pad_maximum_fusion
  213.9 5.5 %copy.29 = f32[1024,1024]{1,0:T(8,128)} copy(f32[1024,1024]{0,1:T(8,128)} %pad_maximum_fusion) | data formatting | bytes 8388608
  219.5 3.7 all-to-all-start.2
  223.3 1.9 fusion.39
  225.7 22.4 %all-to-all-done.2 = bf16[2,512,512]{2,1,0:T(8,128)(2,1)S(1)} async-done(((bf16[2,512,512]{2,1,0:T(8,128)(2,1)}), bf16[2,512,512]{2,1,0:T(8,128)(2,1)S(1)}, u32[]{:S(2)}, u32[]{:S(2)}) %all-to-all-start.2) | async-done | bytes 1048608 | tf_op jit(solution)/shard_map/all_to_all | solution.py:37
  248.6 5.6 %psum.23 = f32[]{:T(128)} all-reduce(f32[]{:T(128)} %reduce_sum.38), channel_id=1, replica_groups=mesh['space'=16,'tensor'=2] {'tensor'}, use_global_device_ids=true, to_apply=%region_6.7 | all-reduce | flops 1 | bytes 8 | tf_op jit(solution)/shard_map/psum | solution.py:66
  254.9 3.9 fusion.37
  258.8 66.0 %reduce-scatter.7.cloned.1.call-done = f32[64,1024]{1,0:T(8,128)} async-done(((f32[1024,1024]{1,0:T(8,128)}), f32[64,1024]{1,0:T(8,128)}) %reduce-scatter.7.cloned.1.call-update) | async-done | bytes 262160
  326.4 59.2 %reduce-scatter.5.cloned.1.call-done = f32[176,64]{0,1:T(8,128)} async-done(((f32[176,1024]{0,1:T(8,128)}), f32[176,64]{0,1:T(8,128)}) %reduce-scatter.5.cloned.1.call-update) | async-done | bytes 45072 | tf_op jit(solution)/shard_map/reduce_scatter | solution.py:73
  (62 shorter events, 9.4 us)
Async XLA Ops:
  7.2 35.2 %all-gather.15.cloned.1.call-start = ((), (), s32[]{:S(2)}) async-start(), calls=%async_computation.10 | async-start | bytes 2752512 | tf_op jit(solution)/shard_map/all_gather | solution.py:52
  7.9 75.8 %all-gather.7.cloned.1.call-start = ((), (), s32[]{:S(2)}) async-start(), calls=%async_computation.5 | async-start | bytes 2752512 | tf_op jit(solution)/shard_map/all_gather | solution.py:55
  45.3 8.1 %copy-start.1 = (bf16[896,2,512]{0,2,1:T(8,128)(2,1)}, bf16[896,2,512]{0,2,1:T(8,128)(2,1)S(1)}, u32[]{:S(2)}) copy-start(bf16[896,2,512]{0,2,1:T(8,128)(2,1)S(1)} %copy.23) | copy-start | bytes 5505028
  45.3 38.5 %copy-start.4 = (bf16[1024,512]{1,0:T(8,128)(2,1)S(1)}, bf16[1024,512]{1,0:T(8,128)(2,1)}, u32[]{:S(2)}) copy-start(bf16[1024,512]{1,0:T(8,128)(2,1)} %param.10) | copy-start | bytes 3145732
  53.4 37.8 %copy-start.3 = (bf16[176,1024]{1,0:T(8,128)(2,1)S(1)}, bf16[176,1024]{1,0:T(8,128)(2,1)}, u32[]{:S(2)}) copy-start(bf16[176,1024]{1,0:T(8,128)(2,1)} %param.11) | copy-start | bytes 1081348
  53.5 69.0 %all-gather.9.cloned.1.call-start = ((), (), s32[]{:S(2)}) async-start(), calls=%async_computation.6 | async-start | bytes 2752512 | tf_op jit(solution)/shard_map/all_gather | solution.py:58
  91.2 5.0 %copy-start.7 = (s32[4,896]{1,0:T(4,128)S(1)}, s32[4,896]{1,0:T(4,128)}, u32[]{:S(2)}) copy-start(s32[4,896]{1,0:T(4,128)} %param.13) | copy-start | bytes 43012
  92.0 74.6 %all-to-all-start = ((bf16[176,2,512]{2,0,1:T(8,128)(2,1)}), bf16[176,2,512]{2,0,1:T(8,128)(2,1)}, u32[]{:S(2)}, u32[]{:S(2)}) async-start(bf16[176,2,512]{2,0,1:T(8,128)(2,1)} %bitcast.41), calls=%async_computation | async-start | bytes 720896 | tf_op jit(solution)/shard_map/all_to_all | solution.py:40
  96.2 106.0 %all-gather.11.cloned.1.call-start = ((), (), s32[]{:S(2)}) async-start(), calls=%async_computation.7 | async-start | bytes 2752512 | tf_op jit(solution)/shard_map/all_gather | solution.py:75
  96.8 0.7 copy-start.8
  166.6 3.8 copy-start.5
  170.4 84.5 %all-gather.13.cloned.1.call-start = ((), (), s32[]{:S(2)}) async-start(), calls=%async_computation.8 | async-start | bytes 2752512 | tf_op jit(solution)/shard_map/all_gather | solution.py:95
  206.8 3.2 copy-start.2
  206.8 3.2 copy-start.6
  206.8 117.9 %reduce-scatter.7.cloned.1.call-start = ((), (), s32[]{:S(2)}) async-start(), calls=%async_computation.11 | async-start | bytes 4456448
  219.5 3.8 copy-start
  219.5 28.6 %all-to-all-start.2 = ((bf16[2,512,512]{2,1,0:T(8,128)(2,1)}), bf16[2,512,512]{2,1,0:T(8,128)(2,1)S(1)}, u32[]{:S(2)}, u32[]{:S(2)}) async-start(bf16[2,512,512]{2,1,0:T(8,128)(2,1)} %bitcast.49), calls=%async_computation.2 | async-start | bytes 2097152 | tf_op jit(solution)/shard_map/all_to_all | solution.py:37
  223.2 162.4 %reduce-scatter.5.cloned.1.call-start = ((), (), s32[]{:S(2)}) async-start(), calls=%async_computation.9 | async-start | bytes 1114112 | tf_op jit(solution)/shard_map/reduce_scatter | solution.py:73
Sparse Core Ops, SparseCore 0:
  9.5 32.8 all-gather.14
  53.6 30.1 all-gather.6
  91.4 31.0 all-gather.8
  170.5 31.6 all-gather.10
  206.9 40.9 all-gather.12
  251.7 73.0 reduce-scatter.6
  328.9 56.6 reduce-scatter.4
